TPU v7x, 32 devices: a whole 2x2x4 slice. The times are simulated.
32 devices in a mesh: batch: 2 (over x), rows: 4 (over z), chan: 4 (over y, core).
Axes of the slice: x: 2, y: 2, z: 4, core: 2. Of those that a mesh axis runs over, the one named last changes fastest.
Arguments:
- images: float32 [16, 24, 16, 32], P('batch', None, ('rows', 'chan')), may hold values from -6 to 6
- shift_mid: float32 [3, 24], replicated, may hold values from -1.75 to 1.75
- gain_mid: float32 [3, 24], replicated, may hold values from -0.3 to 0.3
- lower_mid: float32 [3, 24, 24], replicated, may hold values from -1.25 to 1.25
- upper_mid: float32 [3, 24, 24], replicated, may hold values from -1.25 to 1.25
- diag_mid: float32 [3, 24], replicated, may hold values from -0.3 to 0.3
- first_mid: bfloat16 [3, 9, 12, 512], replicated, may hold values from -0.625 to 0.625
- first_bias_mid: bfloat16 [3, 512], replicated, may hold values from -3 to 3
- second_mid: bfloat16 [3, 512, 512], replicated, may hold values from -0.25 to 0.25
- second_bias_mid: float32 [3, 512], replicated, may hold values from -3 to 3
- third_mid: bfloat16 [3, 9, 512, 24], replicated, may hold values from -0.09375 to 0.09375
- third_bias_mid: float32 [3, 24], replicated, may hold values from -3 to 3
- shift_top: float32 [2, 48], replicated, may hold values from -1.75 to 1.75
- gain_top: float32 [2, 48], replicated, may hold values from -0.3 to 0.3
- lower_top: float32 [2, 48, 48], replicated, may hold values from -0.875 to 0.875
- upper_top: float32 [2, 48, 48], replicated, may hold values from -0.875 to 0.875
- diag_top: float32 [2, 48], replicated, may hold values from -0.3 to 0.3
- first_top: bfloat16 [2, 9, 24, 512], replicated, may hold values from -0.4375 to 0.4375
- first_bias_top: bfloat16 [2, 512], replicated, may hold values from -3 to 3
- second_top: bfloat16 [2, 512, 512], replicated, may hold values from -0.25 to 0.25
- second_bias_top: float32 [2, 512], replicated, may hold values from -3 to 3
- third_top: bfloat16 [2, 9, 512, 48], replicated, may hold values from -0.09375 to 0.09375
- third_bias_top: float32 [2, 48], replicated, may hold values from -3 to 3
Outputs:
- latent_mid: float32 [16, 12, 16, 32], P('batch', None, ('rows', 'chan'))
- latent_top: float32 [16, 48, 8, 16], P(('batch', 'chan'), None, 'rows')
- loglik: float32 [16], P(('batch', 'chan'))
All inputs are finite; a program needn't handle non-finite values.
Results may differ from a plain program's by a relative error of at most 0.008.
Values may be sent and summed in bfloat16 or wider, within the bound.
A program may use at most 64 MiB of HBM per device.

v0:
```python
import functools
import math

import jax
import jax.numpy as jnp
from jax import lax
from jax.experimental import pallas as pl
from jax.experimental.pallas import tpu as pltpu
from jax.sharding import PartitionSpec as P

MESH = pl.DeviceIdType.MESH
LANES = 128
CHUNK = 256
FINE = lax.Precision.HIGHEST
log_two_pi = math.log(2.0 * math.pi)
f32 = jnp.float32
bf16 = jnp.bfloat16


def up8(n):
    return -(-n // 8) * 8


def iota(shape, dim):
    return lax.broadcasted_iota(jnp.int32, shape, dim)


def dot_nt(a, b, precision=None):
    return lax.dot_general(
        a, b, (((1,), (1,)), ((), ())), preferred_element_type=f32, precision=precision
    )


def dot_tn(a, b):
    return lax.dot_general(a, b, (((0,), (0,)), ((), ())), preferred_element_type=f32)


def roll_back(x, amount):
    n = x.shape[1]
    amount = amount % n
    return x if amount == 0 else pltpu.roll(x, n - amount, 1)


def neighbour_masks(n, height, width):
    lane = iota((1, n), 1)
    place = lax.rem(lane, height * width)
    row = lax.div(place, width)
    col = lax.rem(place, width)
    row_ok = {-1: row >= 1, 1: row < height - 1}
    col_ok = {-1: col >= 1, 1: col < width - 1}
    return row_ok, col_ok


def keep(x, ok):
    return jnp.where(ok, x, 0.0)


def spread_taps(q, masks, width):
    row_ok, col_ok = masks
    by_col = {}
    for dc in (-1, 0, 1):
        by_col[dc] = q if dc == 0 else keep(roll_back(q, dc), col_ok[dc])
    taps = []
    for dr in (-1, 0, 1):
        for dc in (-1, 0, 1):
            x = by_col[dc]
            taps.append(x if dr == 0 else keep(roll_back(x, dr * width), row_ok[dr]))
    return jnp.concatenate(taps, axis=0)


def gather_taps(y_ref, channels, n, masks, width):
    row_ok, col_ok = masks
    total = None
    for dc in (-1, 0, 1):
        part = None
        for dr in (-1, 0, 1):
            tap = (dr + 1) * 3 + dc + 1
            y = y_ref[tap * channels : (tap + 1) * channels, :n]
            if dr != 0:
                y = keep(roll_back(y, dr * width), row_ok[dr])
            part = y if part is None else part + y
        if dc != 0:
            part = keep(roll_back(part, dc), col_ok[dc])
        total = part if total is None else total + part
    return total


def mixing(lower, upper, diag_row, gain_row, shift_row, in_map):
    channels = lower.shape[0]
    half = channels // 2
    padded = up8(half)
    i = iota((channels, channels), 0)
    j = iota((channels, channels), 1)
    eye = jnp.where(i == j, 1.0, 0.0)
    low = jnp.where(i > j, lower, 0.0) + eye
    upp = (jnp.where(i < j, upper, 0.0) + eye * jnp.exp(diag_row)) * jnp.exp(gain_row)
    out_map = pad_map(channels)
    rows = jnp.dot(out_map, low, precision=FINE, preferred_element_type=f32)
    mat = jnp.dot(rows, upp, precision=FINE, preferred_element_type=f32)
    bias = jnp.sum(mat * shift_row, axis=1, keepdims=True)
    if in_map is not None:
        mat = dot_nt(mat, in_map, FINE)
    return mat, bias


def pad_map(channels):
    half = channels // 2
    padded = up8(half)
    i = iota((2 * padded, channels), 0)
    j = iota((2 * padded, channels), 1)
    first = (j < half) & (i == j)
    second = (j >= half) & (i - padded == j - half)
    return jnp.where(first | second, 1.0, 0.0)


def squeeze_map(kept, padded):
    i = iota((4 * padded, 4 * kept), 0)
    j = iota((4 * padded, 4 * kept), 1)
    same = (lax.rem(i, padded) == lax.div(j, 4)) & (lax.div(i, padded) == lax.rem(j, 4))
    return jnp.where(same, 1.0, 0.0)


def to_column(row):
    n = row.shape[1]
    eye = iota((n, n), 0) == iota((n, n), 1)
    return jnp.sum(jnp.where(eye, row, 0.0), axis=1, keepdims=True)


def kernel(dims, *refs):
    count = dims[-1]
    sources, refs = refs[:count], refs[count:]
    (mid_out, top_out, lik_out), refs = refs[:3], refs[3:]
    held, refs = refs[:count], refs[count:]
    (
        images,
        shift_mid,
        gain_mid,
        lower_mid,
        upper_mid,
        diag_mid,
        w1_raw,
        first_bias_mid,
        w2_mid,
        second_bias_mid,
        w3_mid,
        third_bias_mid,
        shift_top,
        gain_top,
        lower_top,
        upper_top,
        diag_top,
        w1_top,
        first_bias_top,
        w2_top,
        second_bias_top,
        w3_top,
        third_bias_top,
    ) = held
    (
        outbox,
        inbox,
        w1_mid,
        pick,
        y_scr,
        z_scr,
        z_send,
        z_recv,
        w_sem,
        send_sem,
        recv_sem,
        z_send_sem,
        z_recv_sem,
        t_send,
        t_recv,
        t_send_sem,
        t_recv_sem,
    ) = refs
    n_rows, n_chan, split, height, width, _ = dims
    n_imgs, channels, block = images.shape
    steps_mid = shift_mid.shape[0]
    steps_top = shift_top.shape[0]
    group = n_imgs // n_chan
    peers = n_rows * n_chan
    b = lax.axis_index("batch")
    r = lax.axis_index("rows")
    c = lax.axis_index("chan")
    me = r * n_chan + c
    mine = lax.rem(r, split)
    base = r - mine
    own_imgs = group // split

    def device(row, chan):
        return {"batch": b, "rows": row, "chan": chan}

    barrier = pltpu.get_barrier_semaphore()
    for d in range(1, peers):
        other = lax.rem(me + d, peers)
        pl.semaphore_signal(
            barrier,
            inc=1,
            device_id=device(other // n_chan, lax.rem(other, n_chan)),
            device_id_type=MESH,
        )

    copies = []
    for at in range(count):
        copy = pltpu.make_async_copy(sources[at], held[at], w_sem.at[at])
        copy.start()
        copies.append(copy)
    copies[0].wait()

    per = LANES // block
    slabs = channels // 8
    pieces = [(img, slab) for img in range(own_imgs) for slab in range(slabs)]
    packs = -(-len(pieces) // per)
    for dest in range(n_chan * split):
        rows = []
        for pack in range(packs):
            parts = []
            for img, slab in pieces[pack * per : (pack + 1) * per]:
                parts.append(images[dest * own_imgs + img, slab * 8 : slab * 8 + 8, :])
            while len(parts) < per:
                parts.append(jnp.zeros((8, block), f32))
            rows.append(jnp.concatenate(parts, axis=1))
        outbox[dest] = jnp.concatenate(rows, axis=0).astype(bf16)

    pl.semaphore_wait(barrier, peers - 1)
    sends = []
    for d in range(1, peers):
        other = lax.rem(me + d, peers)
        other_chan = lax.rem(other, n_chan)
        copy = pltpu.make_async_remote_copy(
            src_ref=outbox.at[other_chan * split + lax.rem(other // n_chan, split)],
            dst_ref=inbox.at[me],
            send_sem=send_sem.at[d],
            recv_sem=recv_sem.at[d],
            device_id=device(other // n_chan, other_chan),
            device_id_type=MESH,
        )
        copy.start()
        sends.append(copy)

    inbox[me] = outbox[c * split + mine]

    for copy in copies[1:]:
        copy.wait()
    half = channels // 2
    padded = up8(half)
    top_channels = 4 * half
    mats_mid = []
    for s in range(steps_mid):
        mats_mid.append(
            mixing(
                lower_mid[s],
                upper_mid[s],
                diag_mid[s : s + 1, :],
                gain_mid[s : s + 1, :],
                shift_mid[s : s + 1, :],
                None if s == 0 else pad_map(channels),
            )
        )
    mats_top = []
    for s in range(steps_top):
        mats_top.append(
            mixing(
                lower_top[s],
                upper_top[s],
                diag_top[s : s + 1, :],
                gain_top[s : s + 1, :],
                shift_top[s : s + 1, :],
                squeeze_map(half, padded) if s == 0 else pad_map(top_channels),
            )
        )
    bias3_mid = [to_column(third_bias_mid[s : s + 1, :]) for s in range(steps_mid)]
    bias3_top = [to_column(third_bias_top[s : s + 1, :]) for s in range(steps_top)]
    span = pick.shape[0]
    quarter = span // 4
    to = iota((1, span), 1)
    ij = lax.div(to, quarter)
    cell = lax.rem(to, quarter)
    coarse_w = width // 2
    origin = (2 * lax.div(cell, coarse_w) + lax.div(ij, 2)) * width
    origin = origin + 2 * lax.rem(cell, coarse_w) + lax.rem(ij, 2)
    for k in range(0, span, LANES):
        pick[k : k + LANES, :] = jnp.where(
            iota((LANES, span), 0) + k == origin, 1.0, 0.0
        ).astype(bf16)
    for s in range(steps_mid):
        for tap in range(9):
            w = w1_raw[s, tap].astype(f32)
            if padded > half:
                w = jnp.concatenate([w, jnp.zeros((padded - half, w.shape[1]), f32)], axis=0)
            w1_mid[s, tap * padded : (tap + 1) * padded, :] = w.astype(bf16)
    const_mid = height * width * (jnp.sum(gain_mid[...]) + jnp.sum(diag_mid[...]))
    const_top = (height // 2) * (width // 2) * (jnp.sum(gain_top[...]) + jnp.sum(diag_top[...]))

    for d in range(1, peers):
        source = lax.rem(me + peers - d, peers)
        pltpu.make_async_remote_copy(
            src_ref=outbox.at[0],
            dst_ref=inbox.at[source],
            send_sem=send_sem.at[d],
            recv_sem=recv_sem.at[d],
            device_id=device(r, c),
            device_id_type=MESH,
        ).wait_recv()

    cells = height * width
    n_mid = own_imgs * cells
    columns = []
    letters = [inbox[source].astype(f32) for source in range(peers)]
    for img in range(own_imgs):
        for quad in range(peers // per):
            stack = []
            for slab in range(slabs):
                at = img * slabs + slab
                lo = (at % per) * block
                top = at // per * 8
                parts = [
                    letters[quad * per + j][top : top + 8, lo : lo + block] for j in range(per)
                ]
                stack.append(jnp.concatenate(parts, axis=1))
            columns.append(jnp.concatenate(stack, axis=0))
    state = jnp.concatenate(columns, axis=1)

    def step(state, mat, bias, w1, b1, w2, b2, w3, b3, masks, width, chans):
        n = state.shape[1]
        half_c = chans // 2
        hp = up8(half_c)
        u = jnp.dot(mat, state, precision=FINE, preferred_element_type=f32) + bias
        ua, ub = u[:hp], u[hp:]
        spread = spread_taps(ua, masks, width).astype(bf16)
        size = min(CHUNK, n)
        for at in range(0, n, size):
            h1 = dot_tn(spread[:, at : at + size], w1)
            h1 = jnp.maximum(h1 + b1, 0.0).astype(bf16)
            h2 = jnp.dot(h1, w2[...], preferred_element_type=f32)
            h2 = jnp.maximum(h2 + b2, 0.0).astype(bf16)
            y_scr[: 9 * chans, at : at + size] = dot_nt(w3[...], h2)
        out = gather_taps(y_scr, chans, n, masks, width) + b3
        g = out[:hp] + 2.0
        t = out[half_c:]
        if hp > half_c:
            t = jnp.concatenate([t, jnp.zeros((hp - half_c, n), f32)], axis=0)
        e = jnp.exp(-jnp.abs(g))
        inv = 1.0 / (1.0 + e)
        gate = jnp.where(g >= 0, inv, e * inv)
        logs = jnp.minimum(g, 0.0) - jnp.log(1.0 + e)
        if hp > half_c:
            logs = jnp.where(iota((hp, n), 0) < half_c, logs, 0.0)
        return ua, (ub + t) * gate, logs

    masks = neighbour_masks(n_mid, height, width)
    score = None
    for s in range(steps_mid):
        ua, updated, logs = step(
            state,
            *mats_mid[s],
            w1_mid[s],
            first_bias_mid[s : s + 1, :].astype(f32),
            w2_mid.at[s],
            second_bias_mid[s : s + 1, :],
            w3_mid.at[s],
            bias3_mid[s],
            masks,
            width,
            channels,
        )
        score = logs if score is None else score + logs
        if s < steps_mid - 1:
            state = jnp.concatenate([ua, updated], axis=0)
    score = score - 0.5 * ua * ua
    z_scr[...] = ua
    strip = n_chan * block
    for to_row in range(split):
        for img in range(own_imgs):
            begin = pl.multiple_of(img * cells + (base + to_row) * strip, LANES)
            z_send[to_row, img] = z_scr[:, pl.ds(begin, strip)]

    parts = []
    rest = updated
    for _ in range(3):
        piece = rest.astype(bf16)
        rest = rest - piece.astype(f32)
        parts.append(piece)
    blocks = []
    parts = jnp.concatenate([x.astype(f32) for x in parts], axis=0).astype(bf16)
    for at in range(0, n_mid, span):
        got = jnp.dot(parts[:, at : at + span], pick[...], preferred_element_type=f32)
        total = got[:padded] + got[padded : 2 * padded] + got[2 * padded :]
        blocks.append(
            jnp.concatenate([total[:, k * quarter : (k + 1) * quarter] for k in range(4)], axis=0)
        )
    state = jnp.concatenate(blocks, axis=1)

    team = split * n_chan
    seat = mine * n_chan + c
    z_copies = []
    for d in range(1, team):
        other = lax.rem(seat + d, team)
        copy = pltpu.make_async_remote_copy(
            src_ref=z_send.at[other // n_chan],
            dst_ref=z_recv.at[seat],
            send_sem=z_send_sem.at[d],
            recv_sem=z_recv_sem.at[d],
            device_id=device(base + other // n_chan, lax.rem(other, n_chan)),
            device_id_type=MESH,
        )
        copy.start()
        z_copies.append(copy)
    z_recv[seat] = z_send[mine]

    n_top = n_mid // 4
    masks = neighbour_masks(n_top, height // 2, width // 2)
    score_top = None
    for s in range(steps_top):
        ua, updated, logs = step(
            state,
            *mats_top[s],
            w1_top[s],
            first_bias_top[s : s + 1, :].astype(f32),
            w2_top.at[s],
            second_bias_top[s : s + 1, :],
            w3_top.at[s],
            bias3_top[s],
            masks,
            width // 2,
            top_channels,
        )
        score_top = logs if score_top is None else score_top + logs
        state = jnp.concatenate([ua, updated], axis=0)
    score_top = score_top - 0.5 * (ua * ua + updated * updated)

    top_cells = cells // 4
    own = top_cells // n_rows
    hp = up8(top_channels // 2)
    if hp * 2 > top_channels:
        state = jnp.concatenate([ua[: top_channels // 2], updated[: top_channels // 2]], axis=0)
    flipped = jnp.transpose(state)
    y_scr[: flipped.shape[0], :top_channels] = flipped
    for to_row in range(split):
        for img in range(own_imgs):
            begin = pl.multiple_of(img * top_cells + (base + to_row) * own, 8)
            t_send[to_row, img, :own, :] = y_scr[pl.ds(begin, own), :top_channels]
    fixed = const_mid + const_top - 0.5 * log_two_pi * (half * cells + top_channels * top_cells)
    for img in range(own_imgs):
        total = jnp.sum(score[:, img * cells : (img + 1) * cells])
        total = total + jnp.sum(score_top[:, img * top_cells : (img + 1) * top_cells])
        lik = jnp.full((8, top_channels), (total + fixed) / (channels * cells), f32)
        for to_row in range(split):
            t_send[to_row, img, own:, :] = lik
    t_copies = []
    for d in range(1, split):
        other = lax.rem(mine + d, split)
        copy = pltpu.make_async_remote_copy(
            src_ref=t_send.at[other],
            dst_ref=t_recv.at[mine],
            send_sem=t_send_sem.at[d],
            recv_sem=t_recv_sem.at[d],
            device_id=device(base + other, c),
            device_id_type=MESH,
        )
        copy.start()
        t_copies.append(copy)
    t_recv[mine] = t_send[mine]

    for d in range(1, team):
        pltpu.make_async_remote_copy(
            src_ref=z_send.at[0],
            dst_ref=z_recv.at[lax.rem(seat + team - d, team)],
            send_sem=z_send_sem.at[d],
            recv_sem=z_recv_sem.at[d],
            device_id=device(r, c),
            device_id_type=MESH,
        ).wait_recv()
    for here in range(n_chan):

        @pl.when(c == here)
        def _():
            for source in range(n_chan):
                for img in range(group):
                    sender = img // own_imgs * n_chan + source
                    mid_out[source * group + img] = z_recv[sender, img % own_imgs][
                        :half, here * block : (here + 1) * block
                    ]

    for copy in sends + z_copies:
        copy.wait_send()
    for d in range(1, split):
        pltpu.make_async_remote_copy(
            src_ref=t_send.at[0],
            dst_ref=t_recv.at[lax.rem(mine + split - d, split)],
            send_sem=t_send_sem.at[d],
            recv_sem=t_recv_sem.at[d],
            device_id=device(r, c),
            device_id_type=MESH,
        ).wait_recv()
    for copy in t_copies:
        copy.wait_send()
    for img in range(group):
        letter = t_recv[img // own_imgs, img % own_imgs]
        top_out[img] = letter[:own]
        lik_out[img] = jnp.max(letter[own:])


def deliver(mid, top, lik, mid_out, top_out, lik_out):
    width = mid_out.shape[3]
    for img in range(mid.shape[0]):
        for row in range(mid_out.shape[2]):
            mid_out[img, :, row, :] = mid[img][:, row * width : (row + 1) * width]
    top_out[...] = top[...]
    for img in range(lik.shape[0]):
        lik_out[img] = lik[img]


def body(sizes, images, *params):
    (
        shift_mid,
        gain_mid,
        lower_mid,
        upper_mid,
        diag_mid,
        first_mid,
        first_bias_mid,
        second_mid,
        second_bias_mid,
        third_mid,
        third_bias_mid,
        shift_top,
        gain_top,
        lower_top,
        upper_top,
        diag_top,
        first_top,
        first_bias_top,
        second_top,
        second_bias_top,
        third_top,
        third_bias_top,
    ) = params
    n_rows, n_chan = sizes
    n_imgs, channels, own_rows, width = images.shape
    peers = n_rows * n_chan
    height = own_rows * peers
    block = own_rows * width
    group = n_imgs // n_chan
    half = channels // 2
    padded = up8(half)
    steps_mid, hidden = first_bias_mid.shape
    steps_top, top_channels = shift_top.shape
    cells = height * width
    split = group if n_rows % group == 0 else 1
    own_imgs = group // split
    n_mid = own_imgs * cells
    span = 4 * LANES
    packs = -(-(own_imgs * (channels // 8)) * block // LANES)
    strip = n_chan * block
    own = cells // 4 // n_rows

    w1_top = first_top.reshape(steps_top, -1, hidden)
    w3_mid = third_mid.transpose(0, 1, 3, 2).reshape(steps_mid, -1, hidden)
    w3_top = third_top.transpose(0, 1, 3, 2).reshape(steps_top, -1, hidden)
    operands = (
        images.reshape(n_imgs, channels, block),
        shift_mid,
        gain_mid,
        lower_mid,
        upper_mid,
        diag_mid,
        first_mid,
        first_bias_mid,
        second_mid,
        second_bias_mid,
        w3_mid,
        third_bias_mid,
        shift_top,
        gain_top,
        lower_top,
        upper_top,
        diag_top,
        w1_top,
        first_bias_top,
        second_top,
        second_bias_top,
        w3_top,
        third_bias_top,
    )
    vmem = pl.BlockSpec(memory_space=pltpu.VMEM)
    smem = pl.BlockSpec(memory_space=pltpu.SMEM)
    count = len(operands)
    mid, top, lik = pl.pallas_call(
        functools.partial(kernel, (n_rows, n_chan, split, height, width, count)),
        out_shape=(
            jax.ShapeDtypeStruct((n_imgs, half, block), f32),
            jax.ShapeDtypeStruct((group, own, top_channels), f32),
            jax.ShapeDtypeStruct((group,), f32),
        ),
        in_specs=[pl.BlockSpec(memory_space=pl.ANY)] * count,
        out_specs=(vmem, vmem, smem),
        scratch_shapes=[pltpu.VMEM(x.shape, x.dtype) for x in operands]
        + [
            pltpu.VMEM((n_chan * split, packs * 8, LANES), bf16),
            pltpu.VMEM((peers, packs * 8, LANES), bf16),
            pltpu.VMEM((steps_mid, 9 * padded, hidden), bf16),
            pltpu.VMEM((span, span), bf16),
            pltpu.VMEM((max(9 * top_channels, n_mid // 4), n_mid), f32),
            pltpu.VMEM((padded, n_mid), f32),
            pltpu.VMEM((split, own_imgs, padded, strip), f32),
            pltpu.VMEM((split * n_chan, own_imgs, padded, strip), f32),
            pltpu.SemaphoreType.DMA((count,)),
            pltpu.SemaphoreType.DMA((peers,)),
            pltpu.SemaphoreType.DMA((peers,)),
            pltpu.SemaphoreType.DMA((split * n_chan,)),
            pltpu.SemaphoreType.DMA((split * n_chan,)),
            pltpu.VMEM((split, own_imgs, own + 8, top_channels), f32),
            pltpu.VMEM((split, own_imgs, own + 8, top_channels), f32),
            pltpu.SemaphoreType.DMA((split,)),
            pltpu.SemaphoreType.DMA((split,)),
        ],
        compiler_params=pltpu.CompilerParams(
            collective_id=0, has_side_effects=True, vmem_limit_bytes=56 * 1024 * 1024
        ),
        name="flow",
    )(*operands)
    latent_mid, top, lik = pl.pallas_call(
        deliver,
        out_shape=(
            jax.ShapeDtypeStruct((n_imgs, half, own_rows, width), f32),
            jax.ShapeDtypeStruct(top.shape, f32),
            jax.ShapeDtypeStruct(lik.shape, f32),
        ),
        in_specs=[vmem, vmem, smem],
        out_specs=(vmem, vmem, smem),
        name="deliver",
    )(mid, top, lik)
    latent_top = top.reshape(group, -1, width // 2, top_channels).transpose(0, 3, 1, 2)
    return latent_mid, latent_top, lik


def solution(mesh):
    sizes = (mesh.shape["rows"], mesh.shape["chan"])
    placed = (P("batch", None, ("rows", "chan"), None),) + (P(),) * 22
    return jax.shard_map(
        functools.partial(body, sizes),
        mesh=mesh,
        in_specs=placed,
        out_specs=(
            P("batch", None, ("rows", "chan"), None),
            P(("batch", "chan"), None, "rows", None),
            P(("batch", "chan")),
        ),
        check_vma=False,
    )
```

profile of v0, /device:TPU:0, one launch (start us, length us, event | category | flops | bytes accessed | tf_op | source)
XLA Modules:
  0.0 22.6 jit_solution(1648829144353261218)
XLA Ops:
  0.6 20.4 %flow.1 = (f32[8,12,32]{2,1,0:T(8,128)}, f32[2,32,48]{2,1,0:T(8,128)}, f32[2]{0:T(128)}) custom-call(f32[8,24,32]{2,1,0:T(8,128)} %bitcast.14, f32[3,24]{1,0:T(4,128)} %refs_1_.1, f32[3,24]{1,0:T(4,128)} %refs_2_.1, f32[3,24,24]{2,1,0:T(8,128)} %refs_3_.1, f32[3,24,24]{2,1,0:T(8,128)} %refs_4_.1, f32[3,24]{1,0:T(4,128)} %refs_5_.1, ...), custom_call_target="tpu_custom_call" | custom-call | tf_op jit(solution)/shard_map/flow/pallas_call | solution.py:591
  21.1 1.5 %deliver.1 = (f32[8,12,1,32]{3,2,1,0:T(1,128)}, f32[2,32,48]{2,1,0:T(8,128)}, f32[2]{0:T(128)}) custom-call(f32[8,12,32]{2,1,0:T(8,128)} %get-tuple-element.9.mid, f32[2,32,48]{2,1,0:T(8,128)} %get-tuple-element.10.top, f32[2]{0:T(128)} %get-tuple-element.11.lik), custom_call_target="tpu_custom_call" | custom-call | tf_op jit(solution)/shard_map/deliver/pallas_call | solution.py:625
where the time goes:
time: 22.8 us; the launch traced here: 22.6 us
  Pallas kernels  21.9 us (96%)
  between operations  0.65 us (3%)
    pallas_call x1, Pallas kernels, body(): pl.pallas_call(functools.partial(kernel, (n_rows, n_chan, split, height,...  20.4 us
    pallas_call x1, Pallas kernels, body(): pl.pallas_call(deliver, out_shape=(jax.ShapeDtypeStruct((n_imgs, half, ow...  1.52 us

commit v1 on v0

--- a/solution.py
+++ b/solution.py
@@ -10,7 +10,7 @@
 
 MESH = pl.DeviceIdType.MESH
 LANES = 128
-CHUNK = 256
+CHUNK = 512
 FINE = lax.Precision.HIGHEST
 log_two_pi = math.log(2.0 * math.pi)
 f32 = jnp.float32
@@ -127,34 +127,23 @@
 
 
 def kernel(dims, *refs):
-    count = dims[-1]
-    sources, refs = refs[:count], refs[count:]
+    n_rows, n_chan, split, height, width, places, count = dims
+    sources, refs = refs[: len(places)], refs[len(places) :]
     (mid_out, top_out, lik_out), refs = refs[:3], refs[3:]
     held, refs = refs[:count], refs[count:]
     (
         images,
-        shift_mid,
-        gain_mid,
-        lower_mid,
-        upper_mid,
-        diag_mid,
+        vecs_mid,
+        vecs_top,
+        mats_in_mid,
+        mats_in_top,
         w1_raw,
         first_bias_mid,
-        w2_mid,
+        first_bias_top,
         second_bias_mid,
-        w3_mid,
-        third_bias_mid,
-        shift_top,
-        gain_top,
-        lower_top,
-        upper_top,
-        diag_top,
-        w1_top,
-        first_bias_top,
-        w2_top,
         second_bias_top,
-        w3_top,
-        third_bias_top,
+        w2_all,
+        w13_all,
     ) = held
     (
         outbox,
@@ -165,20 +154,18 @@
         z_scr,
         z_send,
         z_recv,
-        w_sem,
-        send_sem,
-        recv_sem,
-        z_send_sem,
-        z_recv_sem,
         t_send,
         t_recv,
-        t_send_sem,
-        t_recv_sem,
+        t_scr,
+        w_sem,
+        sems,
     ) = refs
-    n_rows, n_chan, split, height, width, _ = dims
+    send_sem, recv_sem, z_send_sem, z_recv_sem, t_send_sem, t_recv_sem = [
+        sems.at[k] for k in range(6)
+    ]
     n_imgs, channels, block = images.shape
-    steps_mid = shift_mid.shape[0]
-    steps_top = shift_top.shape[0]
+    steps_mid = vecs_mid.shape[1]
+    steps_top = vecs_top.shape[1]
     group = n_imgs // n_chan
     peers = n_rows * n_chan
     b = lax.axis_index("batch")
@@ -188,10 +175,37 @@
     mine = lax.rem(r, split)
     base = r - mine
     own_imgs = group // split
+    swap = split > 1 and n_chan % 2 == 0
+
+    def paired(chan):
+        return chan + 1 - 2 * lax.rem(chan, 2) if swap else chan
+
+    work = paired(c)
 
     def device(row, chan):
         return {"batch": b, "rows": row, "chan": chan}
 
+    def fetch(at):
+        where, offset, extent = places[at]
+        target = held[where] if offset is None else held[where].at[offset]
+        if extent is not None:
+            target = held[where].at[pl.ds(offset, extent)]
+        pltpu.make_async_copy(sources[at], target, w_sem.at[where]).start()
+
+    def arrive(where):
+        pltpu.make_async_copy(held[where], held[where], w_sem.at[where]).wait()
+
+    def drain(ref, total, send, recv):
+        return pltpu.make_async_remote_copy(
+            src_ref=ref.at[pl.ds(0, total)],
+            dst_ref=ref.at[pl.ds(0, total)],
+            send_sem=send,
+            recv_sem=recv,
+            device_id=device(r, c),
+            device_id_type=MESH,
+        )
+
+    fetch(0)
     barrier = pltpu.get_barrier_semaphore()
     for d in range(1, peers):
         other = lax.rem(me + d, peers)
@@ -202,12 +216,9 @@
             device_id_type=MESH,
         )
 
-    copies = []
-    for at in range(count):
-        copy = pltpu.make_async_copy(sources[at], held[at], w_sem.at[at])
-        copy.start()
-        copies.append(copy)
-    copies[0].wait()
+    for at in range(1, len(places)):
+        fetch(at)
+    arrive(0)
 
     per = LANES // block
     slabs = channels // 8
@@ -225,25 +236,33 @@
         outbox[dest] = jnp.concatenate(rows, axis=0).astype(bf16)
 
     pl.semaphore_wait(barrier, peers - 1)
-    sends = []
     for d in range(1, peers):
         other = lax.rem(me + d, peers)
         other_chan = lax.rem(other, n_chan)
         copy = pltpu.make_async_remote_copy(
-            src_ref=outbox.at[other_chan * split + lax.rem(other // n_chan, split)],
+            src_ref=outbox.at[paired(other_chan) * split + lax.rem(other // n_chan, split)],
             dst_ref=inbox.at[me],
-            send_sem=send_sem.at[d],
-            recv_sem=recv_sem.at[d],
+            send_sem=send_sem,
+            recv_sem=recv_sem,
             device_id=device(other // n_chan, other_chan),
             device_id_type=MESH,
         )
         copy.start()
-        sends.append(copy)
-
-    inbox[me] = outbox[c * split + mine]
-
-    for copy in copies[1:]:
-        copy.wait()
+
+    inbox[me] = outbox[work * split + mine]
+
+    for where in range(1, count):
+        arrive(where)
+    shift_mid, gain_mid, diag_mid, third_bias_mid = [vecs_mid[k] for k in range(4)]
+    shift_top, gain_top, diag_top, third_bias_top = [vecs_top[k] for k in range(4)]
+    lower_mid, upper_mid = mats_in_mid.at[0], mats_in_mid.at[1]
+    lower_top, upper_top = mats_in_top.at[0], mats_in_top.at[1]
+    deep = w13_all.shape[1]
+    w3_mid = [w13_all.at[s] for s in range(steps_mid)]
+    w1_top = [w13_all.at[steps_mid + s] for s in range(steps_top)]
+    w3_top = [
+        w13_all.at[pl.ds(steps_mid + steps_top + 2 * s, 2)] for s in range(steps_top)
+    ]
     half = channels // 2
     padded = up8(half)
     top_channels = 4 * half
@@ -291,19 +310,11 @@
             if padded > half:
                 w = jnp.concatenate([w, jnp.zeros((padded - half, w.shape[1]), f32)], axis=0)
             w1_mid[s, tap * padded : (tap + 1) * padded, :] = w.astype(bf16)
-    const_mid = height * width * (jnp.sum(gain_mid[...]) + jnp.sum(diag_mid[...]))
-    const_top = (height // 2) * (width // 2) * (jnp.sum(gain_top[...]) + jnp.sum(diag_top[...]))
-
-    for d in range(1, peers):
-        source = lax.rem(me + peers - d, peers)
-        pltpu.make_async_remote_copy(
-            src_ref=outbox.at[0],
-            dst_ref=inbox.at[source],
-            send_sem=send_sem.at[d],
-            recv_sem=recv_sem.at[d],
-            device_id=device(r, c),
-            device_id_type=MESH,
-        ).wait_recv()
+    const_mid = height * width * (jnp.sum(gain_mid) + jnp.sum(diag_mid))
+    const_top = (height // 2) * (width // 2) * (jnp.sum(gain_top) + jnp.sum(diag_top))
+
+    if peers > 1:
+        drain(inbox, peers - 1, send_sem, recv_sem).wait_recv()
 
     cells = height * width
     n_mid = own_imgs * cells
@@ -323,12 +334,37 @@
             columns.append(jnp.concatenate(stack, axis=0))
     state = jnp.concatenate(columns, axis=1)
 
-    def step(state, mat, bias, w1, b1, w2, b2, w3, b3, masks, width, chans):
+    strip = n_chan * block
+    team = split * n_chan
+    seat = mine * n_chan + c
+
+    def share(ua):
+        z_scr[...] = ua
+        for to_row in range(split):
+            for img in range(own_imgs):
+                begin = pl.multiple_of(img * cells + (base + to_row) * strip, LANES)
+                z_send[to_row, img] = z_scr[:, pl.ds(begin, strip)].astype(bf16)
+        for d in range(1, team):
+            other = lax.rem(seat + d, team)
+            copy = pltpu.make_async_remote_copy(
+                src_ref=z_send.at[other // n_chan],
+                dst_ref=z_recv.at[seat],
+                send_sem=z_send_sem,
+                recv_sem=z_recv_sem,
+                device_id=device(base + other // n_chan, lax.rem(other, n_chan)),
+                device_id_type=MESH,
+            )
+            copy.start()
+        z_recv[seat] = z_send[mine]
+
+    def step(state, mat, bias, w1, b1, w2, b2, w3, b3, masks, width, chans, last=False):
         n = state.shape[1]
         half_c = chans // 2
         hp = up8(half_c)
         u = jnp.dot(mat, state, precision=FINE, preferred_element_type=f32) + bias
         ua, ub = u[:hp], u[hp:]
+        if last:
+            share(ua)
         spread = spread_taps(ua, masks, width).astype(bf16)
         size = min(CHUNK, n)
         for at in range(0, n, size):
@@ -336,7 +372,8 @@
             h1 = jnp.maximum(h1 + b1, 0.0).astype(bf16)
             h2 = jnp.dot(h1, w2[...], preferred_element_type=f32)
             h2 = jnp.maximum(h2 + b2, 0.0).astype(bf16)
-            y_scr[: 9 * chans, at : at + size] = dot_nt(w3[...], h2)
+            w3_now = w3[...].reshape(9 * chans, -1)
+            y_scr[: 9 * chans, at : at + size] = dot_nt(w3_now, h2)
         out = gather_taps(y_scr, chans, n, masks, width) + b3
         g = out[:hp] + 2.0
         t = out[half_c:]
@@ -358,24 +395,19 @@
             *mats_mid[s],
             w1_mid[s],
             first_bias_mid[s : s + 1, :].astype(f32),
-            w2_mid.at[s],
+            w2_all.at[s],
             second_bias_mid[s : s + 1, :],
-            w3_mid.at[s],
+            w3_mid[s],
             bias3_mid[s],
             masks,
             width,
             channels,
+            s == steps_mid - 1,
         )
         score = logs if score is None else score + logs
         if s < steps_mid - 1:
             state = jnp.concatenate([ua, updated], axis=0)
     score = score - 0.5 * ua * ua
-    z_scr[...] = ua
-    strip = n_chan * block
-    for to_row in range(split):
-        for img in range(own_imgs):
-            begin = pl.multiple_of(img * cells + (base + to_row) * strip, LANES)
-            z_send[to_row, img] = z_scr[:, pl.ds(begin, strip)]
 
     parts = []
     rest = updated
@@ -393,23 +425,6 @@
         )
     state = jnp.concatenate(blocks, axis=1)
 
-    team = split * n_chan
-    seat = mine * n_chan + c
-    z_copies = []
-    for d in range(1, team):
-        other = lax.rem(seat + d, team)
-        copy = pltpu.make_async_remote_copy(
-            src_ref=z_send.at[other // n_chan],
-            dst_ref=z_recv.at[seat],
-            send_sem=z_send_sem.at[d],
-            recv_sem=z_recv_sem.at[d],
-            device_id=device(base + other // n_chan, lax.rem(other, n_chan)),
-            device_id_type=MESH,
-        )
-        copy.start()
-        z_copies.append(copy)
-    z_recv[seat] = z_send[mine]
-
     n_top = n_mid // 4
     masks = neighbour_masks(n_top, height // 2, width // 2)
     score_top = None
@@ -417,11 +432,11 @@
         ua, updated, logs = step(
             state,
             *mats_top[s],
-            w1_top[s],
+            w1_top[s][...],
             first_bias_top[s : s + 1, :].astype(f32),
-            w2_top.at[s],
+            w2_all.at[steps_mid + s],
             second_bias_top[s : s + 1, :],
-            w3_top.at[s],
+            w3_top[s],
             bias3_top[s],
             masks,
             width // 2,
@@ -436,81 +451,97 @@
     hp = up8(top_channels // 2)
     if hp * 2 > top_channels:
         state = jnp.concatenate([ua[: top_channels // 2], updated[: top_channels // 2]], axis=0)
-    flipped = jnp.transpose(state)
-    y_scr[: flipped.shape[0], :top_channels] = flipped
-    for to_row in range(split):
-        for img in range(own_imgs):
-            begin = pl.multiple_of(img * top_cells + (base + to_row) * own, 8)
-            t_send[to_row, img, :own, :] = y_scr[pl.ds(begin, own), :top_channels]
     fixed = const_mid + const_top - 0.5 * log_two_pi * (half * cells + top_channels * top_cells)
+    high = t_send.shape[2]
+    folds = -(-top_channels // high)
+    if folds * high > top_channels:
+        filler = jnp.zeros((folds * high - top_channels, n_top), f32)
+        state = jnp.concatenate([state, filler], axis=0)
+    t_scr[...] = state
     for img in range(own_imgs):
         total = jnp.sum(score[:, img * cells : (img + 1) * cells])
         total = total + jnp.sum(score_top[:, img * top_cells : (img + 1) * top_cells])
-        lik = jnp.full((8, top_channels), (total + fixed) / (channels * cells), f32)
+        lik = jnp.full((high, own), (total + fixed) / (channels * cells), f32)
+        coarse = lik.astype(bf16).astype(f32)
+        lik = jnp.where(iota((high, own), 0) == 0, coarse, lik - coarse)
         for to_row in range(split):
-            t_send[to_row, img, own:, :] = lik
-    t_copies = []
-    for d in range(1, split):
+            at = img * top_cells + (base + to_row) * own
+            window = t_scr[:, img * top_cells : (img + 1) * top_cells]
+            parts = []
+            for row in range(n_rows):
+                piece = window[:, row * own : (row + 1) * own]
+                parts.append(
+                    jnp.concatenate(
+                        [piece[k * high : (k + 1) * high] for k in range(folds)] + [lik], axis=1
+                    )
+                )
+            chosen = parts[to_row]
+            for start in range(split, n_rows, split):
+                chosen = jnp.where(base == start, parts[start + to_row], chosen)
+            t_send[to_row, img] = chosen.astype(bf16)
+    t_count = split if swap else split - 1
+    for d in range(split - t_count, split):
         other = lax.rem(mine + d, split)
         copy = pltpu.make_async_remote_copy(
             src_ref=t_send.at[other],
             dst_ref=t_recv.at[mine],
-            send_sem=t_send_sem.at[d],
-            recv_sem=t_recv_sem.at[d],
-            device_id=device(base + other, c),
+            send_sem=t_send_sem,
+            recv_sem=t_recv_sem,
+            device_id=device(base + other, work),
             device_id_type=MESH,
         )
         copy.start()
-        t_copies.append(copy)
-    t_recv[mine] = t_send[mine]
-
-    for d in range(1, team):
-        pltpu.make_async_remote_copy(
-            src_ref=z_send.at[0],
-            dst_ref=z_recv.at[lax.rem(seat + team - d, team)],
-            send_sem=z_send_sem.at[d],
-            recv_sem=z_recv_sem.at[d],
-            device_id=device(r, c),
-            device_id_type=MESH,
-        ).wait_recv()
+    if not swap:
+        t_recv[mine] = t_send[mine]
+
+    if team > 1:
+        drain(z_recv, team - 1, z_send_sem, z_recv_sem).wait_recv()
     for here in range(n_chan):
 
         @pl.when(c == here)
         def _():
             for source in range(n_chan):
+                holder = source + 1 - 2 * (source % 2) if swap else source
                 for img in range(group):
-                    sender = img // own_imgs * n_chan + source
-                    mid_out[source * group + img] = z_recv[sender, img % own_imgs][
+                    sender = img // own_imgs * n_chan + holder
+                    at = (source * group + img) * half
+                    mid_out[at : at + half, :] = z_recv[sender, img % own_imgs].astype(f32)[
                         :half, here * block : (here + 1) * block
                     ]
 
-    for copy in sends + z_copies:
-        copy.wait_send()
-    for d in range(1, split):
-        pltpu.make_async_remote_copy(
-            src_ref=t_send.at[0],
-            dst_ref=t_recv.at[lax.rem(mine + split - d, split)],
-            send_sem=t_send_sem.at[d],
-            recv_sem=t_recv_sem.at[d],
-            device_id=device(r, c),
-            device_id_type=MESH,
-        ).wait_recv()
-    for copy in t_copies:
-        copy.wait_send()
+    if peers > 1:
+        drain(inbox, peers - 1, send_sem, recv_sem).wait_send()
+    if team > 1:
+        drain(z_recv, team - 1, z_send_sem, z_recv_sem).wait_send()
+    if t_count > 0:
+        drain(t_recv, t_count, t_send_sem, t_recv_sem).wait()
+    liks = []
+    letters = []
     for img in range(group):
-        letter = t_recv[img // own_imgs, img % own_imgs]
-        top_out[img] = letter[:own]
-        lik_out[img] = jnp.max(letter[own:])
-
-
-def deliver(mid, top, lik, mid_out, top_out, lik_out):
-    width = mid_out.shape[3]
-    for img in range(mid.shape[0]):
-        for row in range(mid_out.shape[2]):
-            mid_out[img, :, row, :] = mid[img][:, row * width : (row + 1) * width]
-    top_out[...] = top[...]
-    for img in range(lik.shape[0]):
-        lik_out[img] = lik[img]
+        letter = t_recv[img // own_imgs, img % own_imgs].astype(f32)
+        letters.append(letter)
+        lik = letter[:2, folds * own : folds * own + 1]
+        liks.append(lik[:1] + lik[1:])
+    flipped = jnp.transpose(jnp.concatenate(letters, axis=0))
+    for img in range(group):
+        for k in range(folds):
+            size = min(high, top_channels - k * high)
+            top_out[img, :, k * high : k * high + size] = flipped[
+                k * own : (k + 1) * own, img * high : img * high + size
+            ]
+    lik_out[...] = jnp.concatenate(liks, axis=1)
+
+
+def deliver(*refs):
+    count = len(refs) // 2
+    sems = refs[-1]
+    copies = [
+        pltpu.make_async_copy(refs[at], refs[count + at], sems.at[at]) for at in range(count)
+    ]
+    for copy in copies:
+        copy.start()
+    for copy in copies:
+        copy.wait()
 
 
 def body(sizes, images, *params):
@@ -556,85 +587,86 @@
     packs = -(-(own_imgs * (channels // 8)) * block // LANES)
     strip = n_chan * block
     own = cells // 4 // n_rows
-
-    w1_top = first_top.reshape(steps_top, -1, hidden)
-    w3_mid = third_mid.transpose(0, 1, 3, 2).reshape(steps_mid, -1, hidden)
-    w3_top = third_top.transpose(0, 1, 3, 2).reshape(steps_top, -1, hidden)
-    operands = (
-        images.reshape(n_imgs, channels, block),
-        shift_mid,
-        gain_mid,
-        lower_mid,
-        upper_mid,
-        diag_mid,
-        first_mid,
-        first_bias_mid,
-        second_mid,
-        second_bias_mid,
-        w3_mid,
-        third_bias_mid,
-        shift_top,
-        gain_top,
-        lower_top,
-        upper_top,
-        diag_top,
-        w1_top,
-        first_bias_top,
-        second_top,
-        second_bias_top,
-        w3_top,
-        third_bias_top,
+    high = -(-top_channels // max(1, LANES // own - 1) // 16) * 16
+    folds = -(-top_channels // high)
+
+    deep = 9 * channels
+    w1_top = first_top.reshape(steps_top, deep, hidden)
+    w3_mid = third_mid.transpose(0, 1, 3, 2).reshape(steps_mid, deep, hidden)
+    w3_top = third_top.transpose(0, 1, 3, 2).reshape(2 * steps_top, deep, hidden)
+    layout = (
+        ((images.reshape(n_imgs, channels, block), None),),
+        tuple((x, k) for k, x in enumerate((shift_mid, gain_mid, diag_mid, third_bias_mid))),
+        tuple((x, k) for k, x in enumerate((shift_top, gain_top, diag_top, third_bias_top))),
+        ((lower_mid, 0), (upper_mid, 1)),
+        ((lower_top, 0), (upper_top, 1)),
+        ((first_mid, None),),
+        ((first_bias_mid, None),),
+        ((first_bias_top, None),),
+        ((second_bias_mid, None),),
+        ((second_bias_top, None),),
+        ((second_mid, 0), (second_top, steps_mid)),
+        ((w3_mid, 0), (w1_top, steps_mid), (w3_top, steps_mid + steps_top)),
     )
+    operands, places, stores = [], [], []
+    for where, entry in enumerate(layout):
+        first = entry[0][0]
+        joined = where >= len(layout) - 2
+        if joined:
+            shape = (sum(x.shape[0] for x, _ in entry),) + first.shape[1:]
+        elif entry[0][1] is None:
+            shape = first.shape
+        else:
+            shape = (len(entry),) + first.shape
+        stores.append(pltpu.VMEM(shape, first.dtype))
+        for x, offset in entry:
+            operands.append(x)
+            places.append((where, offset, x.shape[0] if joined else None))
     vmem = pl.BlockSpec(memory_space=pltpu.VMEM)
-    smem = pl.BlockSpec(memory_space=pltpu.SMEM)
-    count = len(operands)
-    mid, top, lik = pl.pallas_call(
-        functools.partial(kernel, (n_rows, n_chan, split, height, width, count)),
-        out_shape=(
-            jax.ShapeDtypeStruct((n_imgs, half, block), f32),
-            jax.ShapeDtypeStruct((group, own, top_channels), f32),
-            jax.ShapeDtypeStruct((group,), f32),
-        ),
-        in_specs=[pl.BlockSpec(memory_space=pl.ANY)] * count,
-        out_specs=(vmem, vmem, smem),
-        scratch_shapes=[pltpu.VMEM(x.shape, x.dtype) for x in operands]
+    hbm = pl.BlockSpec(memory_space=pl.ANY)
+    count = len(stores)
+    results = [
+        (n_imgs * half, block),
+        (group, own, top_channels),
+        (1, group),
+    ]
+    held = pl.pallas_call(
+        functools.partial(kernel, (n_rows, n_chan, split, height, width, places, count)),
+        out_shape=[pltpu.VMEM(x, f32) for x in results],
+        in_specs=[hbm] * len(operands),
+        out_specs=[vmem] * len(results),
+        scratch_shapes=stores
         + [
             pltpu.VMEM((n_chan * split, packs * 8, LANES), bf16),
             pltpu.VMEM((peers, packs * 8, LANES), bf16),
             pltpu.VMEM((steps_mid, 9 * padded, hidden), bf16),
             pltpu.VMEM((span, span), bf16),
-            pltpu.VMEM((max(9 * top_channels, n_mid // 4), n_mid), f32),
+            pltpu.VMEM((9 * top_channels, n_mid), f32),
             pltpu.VMEM((padded, n_mid), f32),
-            pltpu.VMEM((split, own_imgs, padded, strip), f32),
-            pltpu.VMEM((split * n_chan, own_imgs, padded, strip), f32),
+            pltpu.VMEM((split, own_imgs, padded, strip), bf16),
+            pltpu.VMEM((split * n_chan, own_imgs, padded, strip), bf16),
+            pltpu.VMEM((split, own_imgs, high, (folds + 1) * own), bf16),
+            pltpu.VMEM((split, own_imgs, high, (folds + 1) * own), bf16),
+            pltpu.VMEM((folds * high, n_mid // 4), f32),
             pltpu.SemaphoreType.DMA((count,)),
-            pltpu.SemaphoreType.DMA((peers,)),
-            pltpu.SemaphoreType.DMA((peers,)),
-            pltpu.SemaphoreType.DMA((split * n_chan,)),
-            pltpu.SemaphoreType.DMA((split * n_chan,)),
-            pltpu.VMEM((split, own_imgs, own + 8, top_channels), f32),
-            pltpu.VMEM((split, own_imgs, own + 8, top_channels), f32),
-            pltpu.SemaphoreType.DMA((split,)),
-            pltpu.SemaphoreType.DMA((split,)),
+            pltpu.SemaphoreType.DMA((6,)),
         ],
         compiler_params=pltpu.CompilerParams(
             collective_id=0, has_side_effects=True, vmem_limit_bytes=56 * 1024 * 1024
         ),
         name="flow",
     )(*operands)
-    latent_mid, top, lik = pl.pallas_call(
+    mid, top, lik = pl.pallas_call(
         deliver,
-        out_shape=(
-            jax.ShapeDtypeStruct((n_imgs, half, own_rows, width), f32),
-            jax.ShapeDtypeStruct(top.shape, f32),
-            jax.ShapeDtypeStruct(lik.shape, f32),
-        ),
-        in_specs=[vmem, vmem, smem],
-        out_specs=(vmem, vmem, smem),
+        out_shape=[jax.ShapeDtypeStruct(x, f32) for x in results],
+        in_specs=[vmem] * len(results),
+        out_specs=[hbm] * len(results),
+        scratch_shapes=[pltpu.SemaphoreType.DMA((len(results),))],
         name="deliver",
-    )(mid, top, lik)
+    )(*[pltpu.with_memory_space_constraint(x, pltpu.VMEM) for x in held])
+    latent_mid = mid.reshape(n_imgs, half, own_rows, width)
     latent_top = top.reshape(group, -1, width // 2, top_channels).transpose(0, 3, 1, 2)
-    return latent_mid, latent_top, lik
+    return latent_mid, latent_top, lik.reshape(group)
 
 
 def solution(mesh):

time: 22.8 us -> 19.6 us (0.86)
  Pallas kernels: 21.9 us -> 18.8 us
    pallas_call x1, Pallas kernels: 20.4 us -> 18.1 us  [body(): pl.pallas_call(functools.partial(kernel, (n_rows, n_chan, split, height,...]
    pallas_call x1, Pallas kernels: 1.52 us -> 0.66 us  [body(): pl.pallas_call(deliver, out_shape=[jax.ShapeDtypeStruct(x, f32) for x in...]
where the time goes in v1:
time: 19.6 us; the launch traced here: 19.4 us
  Pallas kernels  18.8 us (96%)
  between operations  0.65 us (3%)
    pallas_call x1, Pallas kernels, body(): pl.pallas_call(functools.partial(kernel, (n_rows, n_chan, split, height,...  18.1 us
    pallas_call x1, Pallas kernels, body(): pl.pallas_call(deliver, out_shape=[jax.ShapeDtypeStruct(x, f32) for x in...  0.66 us

profile of v1, /device:TPU:0, one launch (start us, length us, event | category | flops | bytes accessed | tf_op | source)
XLA Modules:
  0.0 19.4 jit_solution(13291166094859686796)
XLA Ops:
  0.6 18.1 %flow.1 = (f32[96,32]{1,0:T(8,128)S(1)}, f32[2,32,48]{2,1,0:T(8,128)S(1)}, f32[1,2]{1,0:T(1,128)S(1)}) custom-call(f32[8,24,32]{2,1,0:T(8,128)} %bitcast.16, f32[3,24]{1,0:T(4,128)} %refs_1_.1, f32[3,24]{1,0:T(4,128)} %refs_2_.1, f32[3,24]{1,0:T(4,128)} %refs_3_.1, f32[3,24]{1,0:T(4,128)} %refs_4_.1, f32[2,48]{1,0:T(2,128)} %refs_5_.1, f32[2,48]{1,0:T(2,128)} %refs_6_.1, ...), custom_call_target="tpu_custom_call" | custom-call | tf_op jit(solution)/shard_map/flow/pallas_call | solution.py:633
  18.8 0.7 %deliver.1 = (f32[96,32]{1,0:T(8,128)}, f32[2,32,48]{2,1,0:T(8,128)}, f32[1,2]{1,0:T(1,128)}) custom-call(f32[96,32]{1,0:T(8,128)S(1)} %get-tuple-element.9.refs_0_, f32[2,32,48]{2,1,0:T(8,128)S(1)} %get-tuple-element.10.refs_1_, f32[1,2]{1,0:T(1,128)S(1)} %get-tuple-element.11.refs_2_), custom_call_target="tpu_custom_call" | custom-call | tf_op jit(solution)/shard_map/deliver/pallas_call | solution.py:659

commit v2 on v1

--- a/solution.py
+++ b/solution.py
@@ -41,51 +41,76 @@
     return x if amount == 0 else pltpu.roll(x, n - amount, 1)
 
 
-def neighbour_masks(n, height, width):
-    lane = iota((1, n), 1)
-    place = lax.rem(lane, height * width)
-    row = lax.div(place, width)
-    col = lax.rem(place, width)
-    row_ok = {-1: row >= 1, 1: row < height - 1}
-    col_ok = {-1: col >= 1, 1: col < width - 1}
-    return row_ok, col_ok
-
-
 def keep(x, ok):
     return jnp.where(ok, x, 0.0)
 
 
-def spread_taps(q, masks, width):
-    row_ok, col_ok = masks
-    by_col = {}
-    for dc in (-1, 0, 1):
-        by_col[dc] = q if dc == 0 else keep(roll_back(q, dc), col_ok[dc])
+def tiles_of(x):
+    return [x[:, at : at + LANES] for at in range(0, x.shape[1], LANES)]
+
+
+def join(parts):
+    return parts[0] if len(parts) == 1 else jnp.concatenate(parts, axis=1)
+
+
+def shift_cols(x, dc, width):
+    if dc == 0:
+        return x
+    col = lax.rem(iota((1, LANES), 1), width)
+    ok = col < width - 1 if dc > 0 else col >= 1
+    return join([keep(roll_back(tile, dc), ok) for tile in tiles_of(x)])
+
+
+def shift_rows(x, dr, width, cells):
+    if dr == 0:
+        return x
+    strip = lax.div(iota((1, LANES), 1), width)
+    ok = strip < LANES // width - 1 if dr > 0 else strip >= 1
+    moved = []
+    for at in range(0, x.shape[1], cells):
+        tiles = tiles_of(x[:, at : at + cells])
+        edge = tiles[0] if dr > 0 else tiles[-1]
+        edge = keep(roll_back(edge, dr * width), ok)
+        moved += tiles[1:] + [edge] if dr > 0 else [edge] + tiles[:-1]
+    return join(moved)
+
+
+def by_row(x, width, cells):
+    depth = cells // LANES
+    if depth == 1:
+        return x
+    parts = []
+    for at in range(0, x.shape[1], cells):
+        for row in range(cells // width):
+            lo = at + row % depth * LANES + row // depth * width
+            parts.append(x[:, lo : lo + width])
+    return join(parts)
+
+
+def spread_taps(q, width, cells):
+    by_col = {dc: shift_cols(q, dc, width) for dc in (-1, 0, 1)}
     taps = []
     for dr in (-1, 0, 1):
         for dc in (-1, 0, 1):
-            x = by_col[dc]
-            taps.append(x if dr == 0 else keep(roll_back(x, dr * width), row_ok[dr]))
+            taps.append(shift_rows(by_col[dc], dr, width, cells))
     return jnp.concatenate(taps, axis=0)
 
 
-def gather_taps(y_ref, channels, n, masks, width):
-    row_ok, col_ok = masks
+def gather_taps(y_ref, channels, n, width, cells):
     total = None
     for dc in (-1, 0, 1):
         part = None
         for dr in (-1, 0, 1):
             tap = (dr + 1) * 3 + dc + 1
             y = y_ref[tap * channels : (tap + 1) * channels, :n]
-            if dr != 0:
-                y = keep(roll_back(y, dr * width), row_ok[dr])
+            y = shift_rows(y, dr, width, cells)
             part = y if part is None else part + y
-        if dc != 0:
-            part = keep(roll_back(part, dc), col_ok[dc])
+        part = shift_cols(part, dc, width)
         total = part if total is None else total + part
     return total
 
 
-def mixing(lower, upper, diag_row, gain_row, shift_row, in_map):
+def mixing(table, lower, upper, diag_row, gain_row, shift_row, in_map):
     channels = lower.shape[0]
     half = channels // 2
     padded = up8(half)
@@ -98,6 +123,10 @@
     rows = jnp.dot(out_map, low, precision=FINE, preferred_element_type=f32)
     mat = jnp.dot(rows, upp, precision=FINE, preferred_element_type=f32)
     bias = jnp.sum(mat * shift_row, axis=1, keepdims=True)
+    for j in range(channels):
+        table[j] = jnp.broadcast_to(mat[:padded, j : j + 1], (padded, LANES))
+    table[channels] = jnp.broadcast_to(bias[:padded], (padded, LANES))
+    mat, bias = mat[padded:], bias[padded:]
     if in_map is not None:
         mat = dot_nt(mat, in_map, FINE)
     return mat, bias
@@ -149,7 +178,10 @@
         outbox,
         inbox,
         w1_mid,
-        pick,
+        mix_mid,
+        mix_top,
+        s_mid,
+        s_top,
         y_scr,
         z_scr,
         z_send,
@@ -270,6 +302,7 @@
     for s in range(steps_mid):
         mats_mid.append(
             mixing(
+                mix_mid.at[s],
                 lower_mid[s],
                 upper_mid[s],
                 diag_mid[s : s + 1, :],
@@ -282,6 +315,7 @@
     for s in range(steps_top):
         mats_top.append(
             mixing(
+                mix_top.at[s],
                 lower_top[s],
                 upper_top[s],
                 diag_top[s : s + 1, :],
@@ -292,18 +326,6 @@
         )
     bias3_mid = [to_column(third_bias_mid[s : s + 1, :]) for s in range(steps_mid)]
     bias3_top = [to_column(third_bias_top[s : s + 1, :]) for s in range(steps_top)]
-    span = pick.shape[0]
-    quarter = span // 4
-    to = iota((1, span), 1)
-    ij = lax.div(to, quarter)
-    cell = lax.rem(to, quarter)
-    coarse_w = width // 2
-    origin = (2 * lax.div(cell, coarse_w) + lax.div(ij, 2)) * width
-    origin = origin + 2 * lax.rem(cell, coarse_w) + lax.rem(ij, 2)
-    for k in range(0, span, LANES):
-        pick[k : k + LANES, :] = jnp.where(
-            iota((LANES, span), 0) + k == origin, 1.0, 0.0
-        ).astype(bf16)
     for s in range(steps_mid):
         for tap in range(9):
             w = w1_raw[s, tap].astype(f32)
@@ -318,28 +340,30 @@
 
     cells = height * width
     n_mid = own_imgs * cells
+    depth = cells // LANES
+    own_rows = block // width
     columns = []
     letters = [inbox[source].astype(f32) for source in range(peers)]
     for img in range(own_imgs):
-        for quad in range(peers // per):
+        for tile in range(depth):
             stack = []
             for slab in range(slabs):
                 at = img * slabs + slab
-                lo = (at % per) * block
                 top = at // per * 8
-                parts = [
-                    letters[quad * per + j][top : top + 8, lo : lo + block] for j in range(per)
-                ]
-                stack.append(jnp.concatenate(parts, axis=1))
+                parts = []
+                for row in range(tile, height, depth):
+                    lo = (at % per) * block + row % own_rows * width
+                    parts.append(letters[row // own_rows][top : top + 8, lo : lo + width])
+                stack.append(join(parts))
             columns.append(jnp.concatenate(stack, axis=0))
-    state = jnp.concatenate(columns, axis=1)
+    s_mid[0, :channels, :] = join(columns)
 
     strip = n_chan * block
     team = split * n_chan
     seat = mine * n_chan + c
 
     def share(ua):
-        z_scr[...] = ua
+        z_scr[...] = by_row(ua, width, cells)
         for to_row in range(split):
             for img in range(own_imgs):
                 begin = pl.multiple_of(img * cells + (base + to_row) * strip, LANES)
@@ -357,15 +381,27 @@
             copy.start()
         z_recv[seat] = z_send[mine]
 
-    def step(state, mat, bias, w1, b1, w2, b2, w3, b3, masks, width, chans, last=False):
-        n = state.shape[1]
+    def step(held_state, rows, table, mat, bias, w1, b1, w2, b2, w3, b3, width, chans, last=False):
+        n = held_state.shape[1]
+        area = n // own_imgs
         half_c = chans // 2
         hp = up8(half_c)
-        u = jnp.dot(mat, state, precision=FINE, preferred_element_type=f32) + bias
-        ua, ub = u[:hp], u[hp:]
+        spans = range(0, n, LANES)
+        sums = [[None] * 4 for _ in spans]
+        for j in range(chans):
+            row = rows[j]
+            for k, at in enumerate(spans):
+                term = table[j] * held_state[row : row + 1, at : at + LANES]
+                old = sums[k][j % 4]
+                sums[k][j % 4] = term if old is None else old + term
+        ua = join([(x[0] + x[1]) + (x[2] + x[3]) + table[chans] for x in sums])
+        ub = jnp.dot(
+            mat, held_state[: mat.shape[1], :], precision=FINE, preferred_element_type=f32
+        )
+        ub = ub + bias
         if last:
             share(ua)
-        spread = spread_taps(ua, masks, width).astype(bf16)
+        spread = spread_taps(ua, width, area).astype(bf16)
         size = min(CHUNK, n)
         for at in range(0, n, size):
             h1 = dot_tn(spread[:, at : at + size], w1)
@@ -374,7 +410,7 @@
             h2 = jnp.maximum(h2 + b2, 0.0).astype(bf16)
             w3_now = w3[...].reshape(9 * chans, -1)
             y_scr[: 9 * chans, at : at + size] = dot_nt(w3_now, h2)
-        out = gather_taps(y_scr, chans, n, masks, width) + b3
+        out = gather_taps(y_scr, chans, n, width, area) + b3
         g = out[:hp] + 2.0
         t = out[half_c:]
         if hp > half_c:
@@ -387,11 +423,13 @@
             logs = jnp.where(iota((hp, n), 0) < half_c, logs, 0.0)
         return ua, (ub + t) * gate, logs
 
-    masks = neighbour_masks(n_mid, height, width)
+    padded_rows = [j if j < half else padded + j - half for j in range(channels)]
     score = None
     for s in range(steps_mid):
         ua, updated, logs = step(
-            state,
+            s_mid.at[s],
+            list(range(channels)) if s == 0 else padded_rows,
+            mix_mid.at[s],
             *mats_mid[s],
             w1_mid[s],
             first_bias_mid[s : s + 1, :].astype(f32),
@@ -399,38 +437,47 @@
             second_bias_mid[s : s + 1, :],
             w3_mid[s],
             bias3_mid[s],
-            masks,
             width,
             channels,
             s == steps_mid - 1,
         )
         score = logs if score is None else score + logs
         if s < steps_mid - 1:
-            state = jnp.concatenate([ua, updated], axis=0)
+            s_mid[s + 1, :padded, :] = ua
+            s_mid[s + 1, padded : 2 * padded, :] = updated
     score = score - 0.5 * ua * ua
 
-    parts = []
-    rest = updated
-    for _ in range(3):
-        piece = rest.astype(bf16)
-        rest = rest - piece.astype(f32)
-        parts.append(piece)
-    blocks = []
-    parts = jnp.concatenate([x.astype(f32) for x in parts], axis=0).astype(bf16)
-    for at in range(0, n_mid, span):
-        got = jnp.dot(parts[:, at : at + span], pick[...], preferred_element_type=f32)
-        total = got[:padded] + got[padded : 2 * padded] + got[2 * padded :]
-        blocks.append(
-            jnp.concatenate([total[:, k * quarter : (k + 1) * quarter] for k in range(4)], axis=0)
-        )
-    state = jnp.concatenate(blocks, axis=1)
+    coarse_w = width // 2
+    lane = iota((padded, LANES), 1)
+    strip_at = lax.div(lane, coarse_w)
+    corner = lax.div(strip_at, 2) * width + 2 * lax.rem(lane, coarse_w)
+    even = lax.rem(strip_at, 2) == 0
+    for img in range(own_imgs):
+        tiles = tiles_of(updated[:, img * cells : (img + 1) * cells])
+        for tile in range(depth // 4):
+            for i in range(2):
+                for j in range(2):
+                    upper_half = jnp.take_along_axis(tiles[2 * tile + i], corner + j, axis=1)
+                    lower_half = jnp.take_along_axis(
+                        tiles[depth // 2 + 2 * tile + i], corner + j, axis=1
+                    )
+                    at = img * cells // 4 + tile * LANES
+                    top = (2 * i + j) * padded
+                    s_top[0, top : top + padded, at : at + LANES] = jnp.where(
+                        even, upper_half, lower_half
+                    )
 
     n_top = n_mid // 4
-    masks = neighbour_masks(n_top, height // 2, width // 2)
+    squeezed_rows = [j % 4 * padded + j // 4 for j in range(top_channels)]
+    top_half = top_channels // 2
+    top_padded = up8(top_half)
+    top_rows = [j if j < top_half else top_padded + j - top_half for j in range(top_channels)]
     score_top = None
     for s in range(steps_top):
         ua, updated, logs = step(
-            state,
+            s_top.at[s],
+            squeezed_rows if s == 0 else top_rows,
+            mix_top.at[s],
             *mats_top[s],
             w1_top[s][...],
             first_bias_top[s : s + 1, :].astype(f32),
@@ -438,12 +485,14 @@
             second_bias_top[s : s + 1, :],
             w3_top[s],
             bias3_top[s],
-            masks,
-            width // 2,
+            coarse_w,
             top_channels,
         )
         score_top = logs if score_top is None else score_top + logs
-        state = jnp.concatenate([ua, updated], axis=0)
+        if s < steps_top - 1:
+            s_top[s + 1, :top_padded, :] = ua
+            s_top[s + 1, top_padded : 2 * top_padded, :] = updated
+    state = jnp.concatenate([ua, updated], axis=0)
     score_top = score_top - 0.5 * (ua * ua + updated * updated)
 
     top_cells = cells // 4
@@ -457,7 +506,7 @@
     if folds * high > top_channels:
         filler = jnp.zeros((folds * high - top_channels, n_top), f32)
         state = jnp.concatenate([state, filler], axis=0)
-    t_scr[...] = state
+    t_scr[...] = by_row(state, coarse_w, top_cells)
     for img in range(own_imgs):
         total = jnp.sum(score[:, img * cells : (img + 1) * cells])
         total = total + jnp.sum(score_top[:, img * top_cells : (img + 1) * top_cells])
@@ -583,7 +632,6 @@
     split = group if n_rows % group == 0 else 1
     own_imgs = group // split
     n_mid = own_imgs * cells
-    span = 4 * LANES
     packs = -(-(own_imgs * (channels // 8)) * block // LANES)
     strip = n_chan * block
     own = cells // 4 // n_rows
@@ -640,7 +688,10 @@
             pltpu.VMEM((n_chan * split, packs * 8, LANES), bf16),
             pltpu.VMEM((peers, packs * 8, LANES), bf16),
             pltpu.VMEM((steps_mid, 9 * padded, hidden), bf16),
-            pltpu.VMEM((span, span), bf16),
+            pltpu.VMEM((steps_mid, channels + 1, padded, LANES), f32),
+            pltpu.VMEM((steps_top, top_channels + 1, up8(top_channels // 2), LANES), f32),
+            pltpu.VMEM((steps_mid, 2 * padded, n_mid), f32),
+            pltpu.VMEM((steps_top, 4 * padded, n_mid // 4), f32),
             pltpu.VMEM((9 * top_channels, n_mid), f32),
             pltpu.VMEM((padded, n_mid), f32),
             pltpu.VMEM((split, own_imgs, padded, strip), bf16),

time: 19.6 us -> 18.5 us (0.944)
  Pallas kernels: 18.8 us -> 17.7 us
    pallas_call x1, Pallas kernels: 18.1 us -> 17 us  [body(): pl.pallas_call(functools.partial(kernel, (n_rows, n_chan, split, height,...]
where the time goes in v2:
time: 18.5 us; the launch traced here: 18.3 us
  Pallas kernels  17.7 us (96%)
  between operations  0.65 us (4%)
    pallas_call x1, Pallas kernels, body(): pl.pallas_call(functools.partial(kernel, (n_rows, n_chan, split, height,...  17 us
    pallas_call x1, Pallas kernels, body(): pl.pallas_call(deliver, out_shape=[jax.ShapeDtypeStruct(x, f32) for x in...  0.66 us

profile of v2, /device:TPU:0, one launch (start us, length us, event | category | flops | bytes accessed | tf_op | source)
XLA Modules:
  0.0 18.3 jit_solution(15654945797331064094)
XLA Ops:
  0.6 17.0 %flow.1 = (f32[96,32]{1,0:T(8,128)S(1)}, f32[2,32,48]{2,1,0:T(8,128)S(1)}, f32[1,2]{1,0:T(1,128)S(1)}) custom-call(f32[8,24,32]{2,1,0:T(8,128)} %bitcast.16, f32[3,24]{1,0:T(4,128)} %refs_1_.1, f32[3,24]{1,0:T(4,128)} %refs_2_.1, f32[3,24]{1,0:T(4,128)} %refs_3_.1, f32[3,24]{1,0:T(4,128)} %refs_4_.1, f32[2,48]{1,0:T(2,128)} %refs_5_.1, f32[2,48]{1,0:T(2,128)} %refs_6_.1, ...), custom_call_target="tpu_custom_call" | custom-call | tf_op jit(solution)/shard_map/flow/pallas_call | solution.py:681
  17.7 0.7 %deliver.1 = (f32[96,32]{1,0:T(8,128)}, f32[2,32,48]{2,1,0:T(8,128)}, f32[1,2]{1,0:T(1,128)}) custom-call(f32[96,32]{1,0:T(8,128)S(1)} %get-tuple-element.9.refs_0_, f32[2,32,48]{2,1,0:T(8,128)S(1)} %get-tuple-element.10.refs_1_, f32[1,2]{1,0:T(1,128)S(1)} %get-tuple-element.11.refs_2_), custom_call_target="tpu_custom_call" | custom-call | tf_op jit(solution)/shard_map/deliver/pallas_call | solution.py:710

commit v3 on v2

--- a/solution.py
+++ b/solution.py
@@ -53,26 +53,19 @@
     return parts[0] if len(parts) == 1 else jnp.concatenate(parts, axis=1)
 
 
-def shift_cols(x, dc, width):
-    if dc == 0:
-        return x
-    col = lax.rem(iota((1, LANES), 1), width)
-    ok = col < width - 1 if dc > 0 else col >= 1
-    return join([keep(roll_back(tile, dc), ok) for tile in tiles_of(x)])
-
-
-def shift_rows(x, dr, width, cells):
-    if dr == 0:
-        return x
-    strip = lax.div(iota((1, LANES), 1), width)
-    ok = strip < LANES // width - 1 if dr > 0 else strip >= 1
-    moved = []
-    for at in range(0, x.shape[1], cells):
-        tiles = tiles_of(x[:, at : at + cells])
-        edge = tiles[0] if dr > 0 else tiles[-1]
-        edge = keep(roll_back(edge, dr * width), ok)
-        moved += tiles[1:] + [edge] if dr > 0 else [edge] + tiles[:-1]
-    return join(moved)
+def shift(tile, dr, dc, width):
+    if dr == 0 and dc == 0:
+        return tile
+    lane = iota((1, LANES), 1)
+    col = lax.rem(lane, width)
+    strip = lax.div(lane, width)
+    ok = None
+    if dc != 0:
+        ok = col < width - 1 if dc > 0 else col >= 1
+    if dr != 0:
+        row_ok = strip < LANES // width - 1 if dr > 0 else strip >= 1
+        ok = row_ok if ok is None else ok & row_ok
+    return keep(roll_back(tile, dr * width + dc), ok)
 
 
 def by_row(x, width, cells):
@@ -88,26 +81,46 @@
 
 
 def spread_taps(q, width, cells):
-    by_col = {dc: shift_cols(q, dc, width) for dc in (-1, 0, 1)}
+    tiles = tiles_of(q)
+    depth = cells // LANES
     taps = []
+    inside = {dc: [shift(x, 0, dc, width) for x in tiles] for dc in (-1, 0, 1)}
     for dr in (-1, 0, 1):
         for dc in (-1, 0, 1):
-            taps.append(shift_rows(by_col[dc], dr, width, cells))
+            moved = []
+            for k in range(len(tiles)):
+                at = k % depth + dr
+                if 0 <= at < depth:
+                    moved.append(inside[dc][k + dr])
+                else:
+                    moved.append(shift(tiles[k + dr - dr * depth], dr, dc, width))
+            taps.append(join(moved))
     return jnp.concatenate(taps, axis=0)
 
 
 def gather_taps(y_ref, channels, n, width, cells):
-    total = None
-    for dc in (-1, 0, 1):
-        part = None
-        for dr in (-1, 0, 1):
-            tap = (dr + 1) * 3 + dc + 1
-            y = y_ref[tap * channels : (tap + 1) * channels, :n]
-            y = shift_rows(y, dr, width, cells)
-            part = y if part is None else part + y
-        part = shift_cols(part, dc, width)
-        total = part if total is None else total + part
-    return total
+    depth = cells // LANES
+
+    def tap(dr, dc, k):
+        top = ((dr + 1) * 3 + dc + 1) * channels
+        return y_ref[top : top + channels, k * LANES : (k + 1) * LANES]
+
+    sums = []
+    for k in range(n // LANES):
+        total = None
+        for dc in (-1, 1, 0):
+            part = None
+            for dr in (-1, 0, 1):
+                if 0 <= k % depth + dr < depth:
+                    y = tap(dr, dc, k + dr)
+                    part = y if part is None else part + y
+                else:
+                    y = shift(tap(dr, dc, k + dr - dr * depth), dr, dc, width)
+                    total = y if total is None else total + y
+            part = shift(part, 0, dc, width)
+            total = part if total is None else total + part
+        sums.append(total)
+    return join(sums)
 
 
 def mixing(table, lower, upper, diag_row, gain_row, shift_row, in_map):
@@ -129,7 +142,13 @@
     mat, bias = mat[padded:], bias[padded:]
     if in_map is not None:
         mat = dot_nt(mat, in_map, FINE)
-    return mat, bias
+    high = mat.astype(bf16).astype(f32)
+    return jnp.concatenate([high, high, mat - high], axis=1).astype(bf16), bias
+
+
+def halves(x):
+    high = x.astype(bf16).astype(f32)
+    return jnp.concatenate([high, x - high, high], axis=0).astype(bf16)
 
 
 def pad_map(channels):
@@ -189,7 +208,6 @@
         t_send,
         t_recv,
         t_scr,
-        w_sem,
         sems,
     ) = refs
     send_sem, recv_sem, z_send_sem, z_recv_sem, t_send_sem, t_recv_sem = [
@@ -217,16 +235,6 @@
     def device(row, chan):
         return {"batch": b, "rows": row, "chan": chan}
 
-    def fetch(at):
-        where, offset, extent = places[at]
-        target = held[where] if offset is None else held[where].at[offset]
-        if extent is not None:
-            target = held[where].at[pl.ds(offset, extent)]
-        pltpu.make_async_copy(sources[at], target, w_sem.at[where]).start()
-
-    def arrive(where):
-        pltpu.make_async_copy(held[where], held[where], w_sem.at[where]).wait()
-
     def drain(ref, total, send, recv):
         return pltpu.make_async_remote_copy(
             src_ref=ref.at[pl.ds(0, total)],
@@ -237,54 +245,69 @@
             device_id_type=MESH,
         )
 
-    fetch(0)
-    barrier = pltpu.get_barrier_semaphore()
-    for d in range(1, peers):
-        other = lax.rem(me + d, peers)
-        pl.semaphore_signal(
-            barrier,
-            inc=1,
-            device_id=device(other // n_chan, lax.rem(other, n_chan)),
-            device_id_type=MESH,
-        )
-
-    for at in range(1, len(places)):
-        fetch(at)
-    arrive(0)
-
     per = LANES // block
     slabs = channels // 8
     pieces = [(img, slab) for img in range(own_imgs) for slab in range(slabs)]
     packs = -(-len(pieces) // per)
-    for dest in range(n_chan * split):
-        rows = []
-        for pack in range(packs):
-            parts = []
-            for img, slab in pieces[pack * per : (pack + 1) * per]:
-                parts.append(images[dest * own_imgs + img, slab * 8 : slab * 8 + 8, :])
-            while len(parts) < per:
-                parts.append(jnp.zeros((8, block), f32))
-            rows.append(jnp.concatenate(parts, axis=1))
-        outbox[dest] = jnp.concatenate(rows, axis=0).astype(bf16)
-
-    pl.semaphore_wait(barrier, peers - 1)
-    for d in range(1, peers):
-        other = lax.rem(me + d, peers)
-        other_chan = lax.rem(other, n_chan)
-        copy = pltpu.make_async_remote_copy(
-            src_ref=outbox.at[paired(other_chan) * split + lax.rem(other // n_chan, split)],
-            dst_ref=inbox.at[me],
-            send_sem=send_sem,
-            recv_sem=recv_sem,
-            device_id=device(other // n_chan, other_chan),
-            device_id_type=MESH,
-        )
-        copy.start()
-
-    inbox[me] = outbox[work * split + mine]
-
-    for where in range(1, count):
-        arrive(where)
+
+    def gather_all(w_sem):
+        def fetch(at):
+            where, offset, extent = places[at]
+            target = held[where] if offset is None else held[where].at[offset]
+            if extent is not None:
+                target = held[where].at[pl.ds(offset, extent)]
+            pltpu.make_async_copy(sources[at], target, w_sem.at[where]).start()
+
+        def arrive(where):
+            pltpu.make_async_copy(held[where], held[where], w_sem.at[where]).wait()
+
+        for img in range(n_imgs):
+            pltpu.make_async_copy(sources[0].at[img], images.at[img], w_sem.at[0]).start()
+        barrier = pltpu.get_barrier_semaphore()
+        for d in range(1, peers):
+            other = lax.rem(me + d, peers)
+            pl.semaphore_signal(
+                barrier,
+                inc=1,
+                device_id=device(other // n_chan, lax.rem(other, n_chan)),
+                device_id_type=MESH,
+            )
+
+        for at in range(1, len(places)):
+            fetch(at)
+        arrive(0)
+
+        for dest in range(n_chan * split):
+            rows = []
+            for pack in range(packs):
+                parts = []
+                for img, slab in pieces[pack * per : (pack + 1) * per]:
+                    parts.append(images[dest * own_imgs + img, slab * 8 : slab * 8 + 8, :])
+                while len(parts) < per:
+                    parts.append(jnp.zeros((8, block), f32))
+                rows.append(jnp.concatenate(parts, axis=1))
+            outbox[dest] = jnp.concatenate(rows, axis=0).astype(bf16)
+
+        pl.semaphore_wait(barrier, peers - 1)
+        for d in range(1, peers):
+            other = lax.rem(me + d, peers)
+            other_chan = lax.rem(other, n_chan)
+            copy = pltpu.make_async_remote_copy(
+                src_ref=outbox.at[paired(other_chan) * split + lax.rem(other // n_chan, split)],
+                dst_ref=inbox.at[me],
+                send_sem=send_sem,
+                recv_sem=recv_sem,
+                device_id=device(other // n_chan, other_chan),
+                device_id_type=MESH,
+            )
+            copy.start()
+
+        inbox[me] = outbox[work * split + mine]
+
+        for where in range(1, count):
+            arrive(where)
+
+    pl.run_scoped(gather_all, pltpu.SemaphoreType.DMA((count,)))
     shift_mid, gain_mid, diag_mid, third_bias_mid = [vecs_mid[k] for k in range(4)]
     shift_top, gain_top, diag_top, third_bias_top = [vecs_top[k] for k in range(4)]
     lower_mid, upper_mid = mats_in_mid.at[0], mats_in_mid.at[1]
@@ -332,13 +355,16 @@
             if padded > half:
                 w = jnp.concatenate([w, jnp.zeros((padded - half, w.shape[1]), f32)], axis=0)
             w1_mid[s, tap * padded : (tap + 1) * padded, :] = w.astype(bf16)
-    const_mid = height * width * (jnp.sum(gain_mid) + jnp.sum(diag_mid))
-    const_top = (height // 2) * (width // 2) * (jnp.sum(gain_top) + jnp.sum(diag_top))
+    def sum_all(x):
+        return jnp.sum(jnp.sum(x, axis=0, keepdims=True), axis=1, keepdims=True)
+
+    cells = height * width
+    fixed = cells * sum_all(gain_mid + diag_mid) + cells // 4 * sum_all(gain_top + diag_top)
+    fixed = fixed / (channels * cells) - 0.5 * log_two_pi
 
     if peers > 1:
         drain(inbox, peers - 1, send_sem, recv_sem).wait_recv()
 
-    cells = height * width
     n_mid = own_imgs * cells
     depth = cells // LANES
     own_rows = block // width
@@ -381,33 +407,41 @@
             copy.start()
         z_recv[seat] = z_send[mine]
 
-    def step(held_state, rows, table, mat, bias, w1, b1, w2, b2, w3, b3, width, chans, last=False):
+    def blend(held_state, rows, table):
+        sums = []
+        for at in range(0, held_state.shape[1], LANES):
+            parts = [table[len(rows)]]
+            for j in range(len(rows)):
+                term = table[j] * held_state[rows[j] : rows[j] + 1, at : at + LANES]
+                if len(parts) < 4:
+                    parts.append(term)
+                else:
+                    parts[j % 4] = parts[j % 4] + term
+            while len(parts) > 1:
+                parts = [sum(parts[x : x + 2][1:], parts[x]) for x in range(0, len(parts), 2)]
+            sums.append(parts[0])
+        return sums
+
+    def step(held_state, rows, table, ahead, mat, bias, w1, b1, w2, b2, w3, b3, width, chans, last=False):
         n = held_state.shape[1]
         area = n // own_imgs
         half_c = chans // 2
         hp = up8(half_c)
-        spans = range(0, n, LANES)
-        sums = [[None] * 4 for _ in spans]
-        for j in range(chans):
-            row = rows[j]
-            for k, at in enumerate(spans):
-                term = table[j] * held_state[row : row + 1, at : at + LANES]
-                old = sums[k][j % 4]
-                sums[k][j % 4] = term if old is None else old + term
-        ua = join([(x[0] + x[1]) + (x[2] + x[3]) + table[chans] for x in sums])
-        ub = jnp.dot(
-            mat, held_state[: mat.shape[1], :], precision=FINE, preferred_element_type=f32
-        )
-        ub = ub + bias
+        ua = join(blend(held_state, rows, table))
         if last:
             share(ua)
         spread = spread_taps(ua, width, area).astype(bf16)
+        if ahead is not None:
+            ahead[:hp, :] = ua
+        source = halves(held_state[: mat.shape[1] // 3, :])
         size = min(CHUNK, n)
         for at in range(0, n, size):
             h1 = dot_tn(spread[:, at : at + size], w1)
             h1 = jnp.maximum(h1 + b1, 0.0).astype(bf16)
             h2 = jnp.dot(h1, w2[...], preferred_element_type=f32)
             h2 = jnp.maximum(h2 + b2, 0.0).astype(bf16)
+            if at == 0:
+                ub = jnp.dot(mat, source, preferred_element_type=f32) + bias
             w3_now = w3[...].reshape(9 * chans, -1)
             y_scr[: 9 * chans, at : at + size] = dot_nt(w3_now, h2)
         out = gather_taps(y_scr, chans, n, width, area) + b3
@@ -415,21 +449,24 @@
         t = out[half_c:]
         if hp > half_c:
             t = jnp.concatenate([t, jnp.zeros((hp - half_c, n), f32)], axis=0)
-        e = jnp.exp(-jnp.abs(g))
-        inv = 1.0 / (1.0 + e)
-        gate = jnp.where(g >= 0, inv, e * inv)
-        logs = jnp.minimum(g, 0.0) - jnp.log(1.0 + e)
+        gate = 0.5 * jnp.tanh(0.5 * g) + 0.5
+        updated = (ub + t) * gate
+        if ahead is not None:
+            ahead[hp : 2 * hp, :] = updated
+        logs = jnp.minimum(g, 0.0) - jnp.log(1.0 + jnp.exp(-jnp.abs(g)))
         if hp > half_c:
             logs = jnp.where(iota((hp, n), 0) < half_c, logs, 0.0)
-        return ua, (ub + t) * gate, logs
+        return ua, updated, logs
 
     padded_rows = [j if j < half else padded + j - half for j in range(channels)]
     score = None
     for s in range(steps_mid):
+        more = s < steps_mid - 1
         ua, updated, logs = step(
             s_mid.at[s],
             list(range(channels)) if s == 0 else padded_rows,
             mix_mid.at[s],
+            s_mid.at[s + 1] if more else None,
             *mats_mid[s],
             w1_mid[s],
             first_bias_mid[s : s + 1, :].astype(f32),
@@ -442,10 +479,13 @@
             s == steps_mid - 1,
         )
         score = logs if score is None else score + logs
-        if s < steps_mid - 1:
-            s_mid[s + 1, :padded, :] = ua
-            s_mid[s + 1, padded : 2 * padded, :] = updated
     score = score - 0.5 * ua * ua
+
+    def fold(x):
+        tiles = [t[at : at + 8] for t in tiles_of(x) for at in range(0, t.shape[0], 8)]
+        return sum(tiles[1:], tiles[0])
+
+    mid_sums = [fold(score[:, img * cells : (img + 1) * cells]) for img in range(own_imgs)]
 
     coarse_w = width // 2
     lane = iota((padded, LANES), 1)
@@ -474,10 +514,12 @@
     top_rows = [j if j < top_half else top_padded + j - top_half for j in range(top_channels)]
     score_top = None
     for s in range(steps_top):
+        more = s < steps_top - 1
         ua, updated, logs = step(
             s_top.at[s],
             squeezed_rows if s == 0 else top_rows,
             mix_top.at[s],
+            s_top.at[s + 1] if more else None,
             *mats_top[s],
             w1_top[s][...],
             first_bias_top[s : s + 1, :].astype(f32),
@@ -489,9 +531,6 @@
             top_channels,
         )
         score_top = logs if score_top is None else score_top + logs
-        if s < steps_top - 1:
-            s_top[s + 1, :top_padded, :] = ua
-            s_top[s + 1, top_padded : 2 * top_padded, :] = updated
     state = jnp.concatenate([ua, updated], axis=0)
     score_top = score_top - 0.5 * (ua * ua + updated * updated)
 
@@ -500,34 +539,33 @@
     hp = up8(top_channels // 2)
     if hp * 2 > top_channels:
         state = jnp.concatenate([ua[: top_channels // 2], updated[: top_channels // 2]], axis=0)
-    fixed = const_mid + const_top - 0.5 * log_two_pi * (half * cells + top_channels * top_cells)
-    high = t_send.shape[2]
+    high = t_send.shape[2] - 16
+    reach = t_send.shape[3]
     folds = -(-top_channels // high)
     if folds * high > top_channels:
         filler = jnp.zeros((folds * high - top_channels, n_top), f32)
         state = jnp.concatenate([state, filler], axis=0)
     t_scr[...] = by_row(state, coarse_w, top_cells)
     for img in range(own_imgs):
-        total = jnp.sum(score[:, img * cells : (img + 1) * cells])
-        total = total + jnp.sum(score_top[:, img * top_cells : (img + 1) * top_cells])
-        lik = jnp.full((high, own), (total + fixed) / (channels * cells), f32)
-        coarse = lik.astype(bf16).astype(f32)
-        lik = jnp.where(iota((high, own), 0) == 0, coarse, lik - coarse)
+        total = mid_sums[img] + fold(score_top[:, img * top_cells : (img + 1) * top_cells])
+        coarse = total.astype(bf16).astype(f32)
+        lik = jnp.concatenate([coarse, total - coarse], axis=0)
+        if reach > LANES:
+            lik = jnp.concatenate([lik, jnp.zeros((16, reach - LANES), f32)], axis=1)
         for to_row in range(split):
-            at = img * top_cells + (base + to_row) * own
             window = t_scr[:, img * top_cells : (img + 1) * top_cells]
             parts = []
             for row in range(n_rows):
                 piece = window[:, row * own : (row + 1) * own]
-                parts.append(
-                    jnp.concatenate(
-                        [piece[k * high : (k + 1) * high] for k in range(folds)] + [lik], axis=1
-                    )
-                )
+                pieces = [piece[k * high : (k + 1) * high] for k in range(folds)]
+                if reach > folds * own:
+                    pieces.append(jnp.zeros((high, reach - folds * own), f32))
+                parts.append(join(pieces))
             chosen = parts[to_row]
             for start in range(split, n_rows, split):
                 chosen = jnp.where(base == start, parts[start + to_row], chosen)
-            t_send[to_row, img] = chosen.astype(bf16)
+            t_send[to_row, img, :high] = chosen.astype(bf16)
+            t_send[to_row, img, high:] = lik.astype(bf16)
     t_count = split if swap else split - 1
     for d in range(split - t_count, split):
         other = lax.rem(mine + d, split)
@@ -568,9 +606,10 @@
     letters = []
     for img in range(group):
         letter = t_recv[img // own_imgs, img % own_imgs].astype(f32)
-        letters.append(letter)
-        lik = letter[:2, folds * own : folds * own + 1]
-        liks.append(lik[:1] + lik[1:])
+        letters.append(letter[:high])
+        lik = letter[high:, :LANES]
+        lik = jnp.sum(jnp.sum(lik, axis=0, keepdims=True), axis=1, keepdims=True)
+        liks.append(lik / (channels * cells) + fixed)
     flipped = jnp.transpose(jnp.concatenate(letters, axis=0))
     for img in range(group):
         for k in range(folds):
@@ -635,7 +674,7 @@
     packs = -(-(own_imgs * (channels // 8)) * block // LANES)
     strip = n_chan * block
     own = cells // 4 // n_rows
-    high = -(-top_channels // max(1, LANES // own - 1) // 16) * 16
+    high = -(-top_channels // max(1, LANES // own) // 16) * 16
     folds = -(-top_channels // high)
 
     deep = 9 * channels
@@ -696,10 +735,9 @@
             pltpu.VMEM((padded, n_mid), f32),
             pltpu.VMEM((split, own_imgs, padded, strip), bf16),
             pltpu.VMEM((split * n_chan, own_imgs, padded, strip), bf16),
-            pltpu.VMEM((split, own_imgs, high, (folds + 1) * own), bf16),
-            pltpu.VMEM((split, own_imgs, high, (folds + 1) * own), bf16),
+            pltpu.VMEM((split, own_imgs, high + 16, max(LANES, folds * own)), bf16),
+            pltpu.VMEM((split, own_imgs, high + 16, max(LANES, folds * own)), bf16),
             pltpu.VMEM((folds * high, n_mid // 4), f32),
-            pltpu.SemaphoreType.DMA((count,)),
             pltpu.SemaphoreType.DMA((6,)),
         ],
         compiler_params=pltpu.CompilerParams(

time: 18.5 us -> 17.9 us (0.968)
  Pallas kernels: 17.7 us -> 17.1 us
    pallas_call x1, Pallas kernels: 17 us -> 16.4 us  [body(): pl.pallas_call(functools.partial(kernel, (n_rows, n_chan, split, height,...]
where the time goes in v3:
time: 17.9 us; the launch traced here: 17.7 us
  Pallas kernels  17.1 us (96%)
  between operations  0.65 us (4%)
    pallas_call x1, Pallas kernels, body(): pl.pallas_call(functools.partial(kernel, (n_rows, n_chan, split, height,...  16.4 us
    pallas_call x1, Pallas kernels, body(): pl.pallas_call(deliver, out_shape=[jax.ShapeDtypeStruct(x, f32) for x in...  0.66 us

profile of v3, /device:TPU:0, one launch (start us, length us, event | category | flops | bytes accessed | tf_op | source)
XLA Modules:
  0.0 17.7 jit_solution(2365058748459004272)
XLA Ops:
  0.6 16.4 %flow.1 = (f32[96,32]{1,0:T(8,128)S(1)}, f32[2,32,48]{2,1,0:T(8,128)S(1)}, f32[1,2]{1,0:T(1,128)S(1)}) custom-call(f32[8,24,32]{2,1,0:T(8,128)} %bitcast.16, f32[3,24]{1,0:T(4,128)} %refs_1_.1, f32[3,24]{1,0:T(4,128)} %refs_2_.1, f32[3,24]{1,0:T(4,128)} %refs_3_.1, f32[3,24]{1,0:T(4,128)} %refs_4_.1, f32[2,48]{1,0:T(2,128)} %refs_5_.1, f32[2,48]{1,0:T(2,128)} %refs_6_.1, ...), custom_call_target="tpu_custom_call" | custom-call | tf_op jit(solution)/shard_map/flow/pallas_call | solution.py:720
  17.1 0.7 %deliver.1 = (f32[96,32]{1,0:T(8,128)}, f32[2,32,48]{2,1,0:T(8,128)}, f32[1,2]{1,0:T(1,128)}) custom-call(f32[96,32]{1,0:T(8,128)S(1)} %get-tuple-element.9.refs_0_, f32[2,32,48]{2,1,0:T(8,128)S(1)} %get-tuple-element.10.refs_1_, f32[1,2]{1,0:T(1,128)S(1)} %get-tuple-element.11.refs_2_), custom_call_target="tpu_custom_call" | custom-call | tf_op jit(solution)/shard_map/deliver/pallas_call | solution.py:748
